TPU v7x, 32 devices: a whole 2x2x4 slice. The times are simulated.
32 devices in a mesh: dp: 8 (over z, x), ctx: 4 (over y, core).
Axes of the slice: x: 2, y: 2, z: 4, core: 2. Of those that a mesh axis runs over, the one named last changes fastest.
Arguments:
- queries: bfloat16 [8, 1024, 2048], P('dp', 'ctx'), may hold values from -100 to 100
- keys: bfloat16 [8, 1024, 512], P('dp', 'ctx'), may hold values from -4 to 4
- values: bfloat16 [8, 1024, 512], P('dp', 'ctx'), may hold values from -6 to 6
- segments: int32 [8, 1024], P('dp', 'ctx'), may hold values from 0 to 7, never falling along the last dimension, each value on 1 to 512 neighbouring positions
Outputs:
- attended: bfloat16 [8, 1024, 2048], P('dp', 'ctx')
Inputs may be any that keep to these rules, and one draw needn't show every extreme that they name: `segments`: document numbers never fall along a packed batch, every one of the 8 documents is present, and each document has at most 512 tokens; some document has exactly 512.
All inputs are finite; a program needn't handle non-finite values.
Results may differ from a plain program's by a relative error of at most 0.0053.
Values may be sent and summed in bfloat16 or wider, within the bound.
A program may use at most 192 MiB of HBM per device.

v0:
```python
import functools
import math

import jax
import jax.numpy as jnp
from jax import lax
from jax.experimental import pallas as pl
from jax.experimental.pallas import tpu as pltpu
from jax.sharding import PartitionSpec as P

HK = 4
HD = 128
THETA = 500000.0
LANES = 128
MASKED = -1e30
F32 = jnp.float32
BF16 = jnp.bfloat16


def sin_cos(angle):
    turns = jnp.floor(angle * (2.0 / math.pi) + 0.5)
    rest = angle - turns * 1.5703125
    rest = rest - turns * 4.837512969970703125e-4
    rest = rest - turns * 7.54978995489188216e-8
    square = rest * rest
    sine = rest + rest * square * (
        -1.6666654611e-1 + square * (8.3321608736e-3 + square * -1.9515295891e-4)
    )
    cosine = (
        1.0
        - 0.5 * square
        + square * square * (4.166664568298827e-2 + square * (-1.388731625493765e-3 + square * 2.443315711809948e-5))
    )
    quarter = turns - 4.0 * jnp.floor(turns * 0.25)
    odd = (quarter == 1.0) | (quarter == 3.0)
    sin_out = jnp.where(odd, cosine, sine)
    cos_out = jnp.where(odd, sine, cosine)
    sin_out = jnp.where(quarter >= 2.0, -sin_out, sin_out)
    cos_out = jnp.where((quarter == 1.0) | (quarter == 2.0), -cos_out, cos_out)
    return sin_out, cos_out


def frequencies():
    index = lax.broadcasted_iota(jnp.int32, (1, HD), 1) % (HD // 2)
    result = jnp.ones((1, HD), F32)
    bit = 1
    while bit < HD // 2:
        factor = math.exp(-math.log(THETA) * 2.0 * bit / HD)
        result = result * jnp.where((index // bit) % 2 == 1, F32(factor), F32(1.0))
        bit *= 2
    return result


def turned(block, cosine, sine):
    block = block.astype(F32)
    return (block * cosine + pltpu.roll(block, HD // 2, 1) * sine).astype(BF16)


def kernel(
    count, hops, q_ref, k_ref, v_ref, seg_ref, out_ref,
    q_own, kwin, vwin, segwin, krot, qrot, weights, denoms, sines, cosines, bias,
    q_sem, seg_sem, own_sem, seg_send, seg_recv, send, recv, forward,
):
    me = lax.axis_index("ctx")
    rows = q_own.shape[0]
    span = bias.shape[2]
    group = qrot.shape[0] // HK
    windows = (kwin, vwin)

    def block(which, head, distance):
        return windows[which].at[head, pl.ds((hops - distance) * rows, rows)]

    own_copies = [
        [
            pltpu.make_async_copy(
                ref.at[0, :, pl.ds(head * HD, HD)], block(which, head, 0), own_sem.at[which, head]
            )
            for head in range(HK)
        ]
        for which, ref in enumerate((k_ref, v_ref))
    ]
    seg_copy = pltpu.make_async_copy(seg_ref, segwin.at[hops], seg_sem)
    q_copy = pltpu.make_async_copy(q_ref.at[0], q_own, q_sem)
    seg_copy.start()
    for which in range(2):
        for head in range(HK):
            own_copies[which][head].start()
    q_copy.start()

    barrier = pltpu.get_barrier_semaphore()
    for distance in range(1, hops + 1):
        @pl.when(me + distance < count)
        def _():
            pl.semaphore_signal(barrier, inc=1, device_id={"ctx": me + distance})

        @pl.when(me >= distance)
        def _():
            pl.semaphore_signal(barrier, inc=1, device_id={"ctx": me - distance})
    pl.semaphore_wait(barrier, jnp.minimum(me, hops) + jnp.minimum(count - 1 - me, hops))

    def seg_out(distance):
        return pltpu.make_async_remote_copy(
            src_ref=segwin.at[hops], dst_ref=segwin.at[hops - distance],
            send_sem=seg_send.at[distance - 1], recv_sem=seg_recv.at[distance - 1],
            device_id={"ctx": me + distance},
        )

    def block_out(which, head, distance):
        return pltpu.make_async_remote_copy(
            src_ref=block(which, head, 0), dst_ref=block(which, head, distance),
            send_sem=send.at[which, head, distance - 1], recv_sem=recv.at[which, head, distance - 1],
            device_id={"ctx": me + distance},
        )

    def block_on(which, head, distance):
        return pltpu.make_async_remote_copy(
            src_ref=block(which, head, distance), dst_ref=block(which, head, distance + 1),
            send_sem=forward.at[which, head, distance - 1], recv_sem=recv.at[which, head, distance],
            device_id={"ctx": me + 1},
        )

    def goes_out(distance):
        direct = me + distance < count
        if distance > 1:
            direct = direct & ((me + distance) % 2 == 0)
        return direct

    def goes_on(distance):
        return (me % 2 == 0) & (me >= distance) & (me + 1 < count)

    seg_copy.wait()
    for distance in range(1, hops + 1):
        @pl.when(me + distance < count)
        def _():
            seg_out(distance).start()
    for which in range(2):
        for head in range(HK):
            own_copies[which][head].wait()

            @pl.when(goes_out(1))
            def _():
                block_out(which, head, 1).start()
    for distance in range(2, hops + 1):
        @pl.when(goes_out(distance))
        def _():
            for which in range(2):
                for head in range(HK):
                    if distance == 2:
                        block_out(which, head, 1).wait_send()
                    block_out(which, head, distance).start()

    for distance in range(1, hops + 1):
        @pl.when(me < distance)
        def _():
            empty = jnp.zeros((HK, rows, HD), BF16)
            kwin[:, pl.ds((hops - distance) * rows, rows)] = empty
            vwin[:, pl.ds((hops - distance) * rows, rows)] = empty
            segwin[hops - distance] = jnp.full((1, rows), -1, jnp.int32)

    for distance in range(1, hops + 1):
        @pl.when(me >= distance)
        def _():
            seg_out(distance).wait_recv()

    freq = frequencies()
    lane = lax.broadcasted_iota(jnp.int32, (rows, LANES), 1)
    row = lax.broadcasted_iota(jnp.int32, (rows, LANES), 0)
    sign = jnp.where(lane < HD // 2, F32(-1.0), F32(1.0))
    ones = jnp.ones((LANES, LANES), BF16)
    pieces = []
    for index in range(hops + 1):
        seg_row = segwin[index].astype(F32)
        pieces += [seg_row[:, at:at + LANES] for at in range(0, rows, LANES)]
    for index in range(hops + 1):
        column = jnp.broadcast_to(segwin[index].astype(F32), (LANES, rows)).T
        smaller = jnp.zeros((rows, LANES), F32)
        for piece in pieces:
            smaller = smaller + jnp.where(piece < column, F32(1.0), F32(0.0))
        start = jnp.dot(smaller.astype(BF16), ones, preferred_element_type=F32)
        position = (row + index * rows).astype(F32) - start
        sine, cosine = sin_cos(position * freq)
        sines[index] = sine * sign
        cosines[index] = cosine
        if index == hops:
            last = (row + hops * rows).astype(F32)
            for tile in range(rows // LANES):
                mine = slice(tile * LANES, (tile + 1) * LANES)
                for at in range(0, span, LANES):
                    spot = (lane[mine] + (at + tile * LANES)).astype(F32)
                    bias[tile, :, at:at + LANES] = jnp.where(
                        (spot >= start[mine]) & (spot <= last[mine]), F32(0.0), F32(MASKED)
                    )

    q_copy.wait()

    @pl.loop(0, qrot.shape[0])
    def _(head):
        at = pl.ds(pl.multiple_of(head * HD, HD), HD)
        qrot[head] = turned(q_own[:, at], cosines[hops], sines[hops])

    scale = F32(math.log2(math.e) / math.sqrt(HD))

    def arrive(head, distance, which):
        @pl.when(me >= distance)
        def _():
            block_out(which, head, distance).wait_recv()
        if distance < hops:
            @pl.when(goes_on(distance))
            def _():
                block_on(which, head, distance).start()

    @pl.loop(0, HK)
    def _(head):
        for distance in range(1, hops + 1):
            arrive(head, distance, 0)
        for index in range(hops + 1):
            at = pl.ds(index * rows, rows)
            krot[at] = turned(kwin[head, at], cosines[index], sines[index])

        for part in range(group):
            for tile in range(rows // LANES):
                mine = slice(tile * LANES, (tile + 1) * LANES)
                seen = pl.ds(tile * LANES, span)
                scores = lax.dot_general(
                    qrot[head * group + part, mine], krot[seen], (((1,), (1,)), ((), ())),
                    preferred_element_type=F32,
                ) + bias[tile]
                top = jnp.max(scores, axis=1, keepdims=True)
                weight = jnp.exp2((scores - top) * scale)
                denoms[head * group + part, mine] = jnp.broadcast_to(
                    jnp.sum(weight, axis=1, keepdims=True), (LANES, LANES)
                )
                weights[head * group + part, mine] = weight.astype(BF16)

    for distance in range(1, hops):
        arrive(0, distance, 1)

    @pl.loop(0, HK)
    def _(head):
        @pl.when(head + 1 < HK)
        def _():
            for distance in range(1, hops):
                arrive(head + 1, distance, 1)

        arrive(head, hops, 1)

        for part in range(group):
            for tile in range(rows // LANES):
                mine = slice(tile * LANES, (tile + 1) * LANES)
                seen = pl.ds(tile * LANES, span)
                total = jnp.dot(weights[head * group + part, mine], vwin[head, seen], preferred_element_type=F32)
                at = pl.ds(pl.multiple_of((head * group + part) * HD, HD), HD)
                out_ref[0, mine, at] = (total / denoms[head * group + part, mine]).astype(BF16)

    for distance in range(1, hops + 1):
        @pl.when(me + distance < count)
        def _():
            seg_out(distance).wait_send()
        unsent = goes_out(distance)
        if distance == 1 and hops > 1:
            unsent = unsent & jnp.logical_not(goes_out(2))
        for which in range(2):
            for head in range(HK):
                @pl.when(unsent)
                def _():
                    block_out(which, head, distance).wait_send()
                if distance < hops:
                    @pl.when(goes_on(distance))
                    def _():
                        block_on(which, head, distance).wait_send()


def body(queries, keys, values, segments):
    count = lax.axis_size("ctx")
    hops = count // 2
    rows = queries.shape[1]
    width = (hops + 1) * rows
    span = hops * rows + LANES
    heads = queries.shape[2] // HD
    group = heads // HK
    anywhere = pl.BlockSpec(memory_space=pltpu.HBM)
    dma = pltpu.SemaphoreType.DMA
    return pl.pallas_call(
        functools.partial(kernel, count, hops),
        out_shape=pltpu.VMEM(queries.shape, BF16),
        in_specs=[anywhere] * 4,
        out_specs=pl.BlockSpec(memory_space=pltpu.VMEM),
        scratch_shapes=[
            pltpu.VMEM((rows, heads * HD), BF16),
            pltpu.VMEM((HK, width, HD), BF16),
            pltpu.VMEM((HK, width, HD), BF16),
            pltpu.VMEM((hops + 1, 1, rows), jnp.int32),
            pltpu.VMEM((width, HD), BF16),
            pltpu.VMEM((heads, rows, HD), BF16),
            pltpu.VMEM((heads, rows, span), BF16),
            pltpu.VMEM((heads, rows, LANES), F32),
            pltpu.VMEM((hops + 1, rows, HD), F32),
            pltpu.VMEM((hops + 1, rows, HD), F32),
            pltpu.VMEM((rows // LANES, LANES, span), F32),
            dma, dma, dma((2, HK)),
            dma((hops,)), dma((hops,)),
            dma((2, HK, hops)), dma((2, HK, hops)), dma((2, HK, hops)),
        ],
        compiler_params=pltpu.CompilerParams(
            collective_id=0, has_side_effects=True, vmem_limit_bytes=60 * 1024 * 1024
        ),
        name="attend",
    )(queries, keys, values, segments)


def solution(mesh):
    placed = (P("dp", "ctx", None), P("dp", "ctx", None), P("dp", "ctx", None), P("dp", "ctx"))
    return jax.shard_map(
        body, mesh=mesh, in_specs=placed, out_specs=P("dp", "ctx", None), check_vma=False
    )
```

profile of v0, /device:TPU:21, one launch (start us, length us, event | category | flops | bytes accessed | tf_op | source)
XLA Modules:
  0.0 16.9 jit_solution(3045473593503038852)
XLA Ops:
  0.0 15.9 %attend.1 = bf16[1,256,2048]{2,1,0:T(8,128)(2,1)S(1)} custom-call(bf16[1,256,2048]{2,1,0:T(8,128)(2,1)} %q_ref.1, bf16[1,256,512]{2,1,0:T(8,128)(2,1)} %k_ref.1, bf16[1,256,512]{2,1,0:T(8,128)(2,1)} %v_ref.1, s32[1,256]{1,0:T(1,128)} %seg_ref.1), custom_call_target="tpu_custom_call" | custom-call | tf_op jit(solution)/shard_map/attend/pallas_call | solution.py:283
  15.9 1.0 %copy.6 = bf16[1,256,2048]{2,1,0:T(8,128)(2,1)} copy(bf16[1,256,2048]{2,1,0:T(8,128)(2,1)S(1)} %attend.1) | data formatting | bytes 2097152
where the time goes:
time: 17.1 us; the launch traced here: 16.9 us
  Pallas kernels  15.9 us (93%)
  local copies, waits for them, and re-layouts  0.97 us (6%)
    pallas_call x1, Pallas kernels, body(): pl.pallas_call(functools.partial(kernel, count, hops), out_shape=pltpu.VM...  15.9 us
    unnamed x1, local copies, waits for them, and re-layouts  0.97 us

commit v1 on v0

--- a/solution.py
+++ b/solution.py
@@ -270,6 +270,545 @@
                         block_on(which, head, distance).wait_send()
 
 
+def relay_kernel(
+    q_ref, k_ref, v_ref, seg_ref, out_ref,
+    q_own, win, segwin, krot, vturn, qrot, tops, totals, sines, cosines, bias,
+    q_in, mix, lse_out, lse_in, q_sine, q_cosine, q_bias, mark, q_next, next_rot, next_bias, next_out,
+    q_sem, seg_sem, own_sem, seg_send, seg_recv, back_send, back_recv, own_send, own_recv,
+    near_send, near_recv, mix_send, mix_recv, lse_send, lse_recv, q_send, q_recv,
+    help_send, help_recv, give_send, give_recv,
+):
+    me = lax.axis_index("ctx")
+    count = lax.axis_size("ctx")
+    rows = q_own.shape[0]
+    heads = q_in.shape[0]
+    group = heads // HK
+    scale = F32(math.log2(math.e) / math.sqrt(HD))
+
+    def blocks(first, last):
+        if isinstance(first, int):
+            return pl.ds(first * LANES, (last - first) * LANES)
+        return pl.ds(pl.multiple_of(first * LANES, LANES), LANES)
+
+    def columns(head):
+        return pl.ds(head * HD if isinstance(head, int) else pl.multiple_of(head * HD, HD), HD)
+
+    every = [(which, head) for head in range(HK) for which in range(2)]
+    own_copies = {
+        (which, head, tile): pltpu.make_async_copy(
+            (k_ref, v_ref)[which].at[0, blocks(tile, tile + 1), columns(head)],
+            win.at[which, head, blocks(4 + tile, 5 + tile)], own_sem.at[which, head, tile],
+        )
+        for which, head in every
+        for tile in range(2)
+    }
+    seg_copy = pltpu.make_async_copy(seg_ref, segwin.at[2], seg_sem)
+    q_copies = [
+        pltpu.make_async_copy(
+            q_ref.at[0, blocks(tile, tile + 1)], q_own.at[blocks(tile, tile + 1)], q_sem.at[tile]
+        )
+        for tile in range(2)
+    ]
+    tail = pl.ds((HK - 1) * group * HD, group * HD)
+    keep_copy = pltpu.make_async_copy(q_ref.at[0, :, tail], q_own.at[:, tail], q_sem.at[0])
+    seg_copy.start()
+
+    barrier = pltpu.get_barrier_semaphore()
+
+    def greet(step, here):
+        @pl.when(here)
+        def _():
+            pl.semaphore_signal(barrier, inc=1, device_id={"ctx": me + step})
+
+    greet(1, me + 1 < count)
+    greet(-1, me >= 1)
+    greet(2, me + 2 < count)
+    greet(-2, me >= 2)
+
+    pl.semaphore_wait(barrier, jnp.minimum(me, 2) + jnp.minimum(count - 1 - me, 2))
+
+    def remote(source, target, sent, received, there):
+        return pltpu.make_async_remote_copy(
+            src_ref=source, dst_ref=target, send_sem=sent, recv_sem=received, device_id={"ctx": there}
+        )
+
+    def seg_out(distance):
+        return remote(
+            segwin.at[2], segwin.at[2 - distance], seg_send.at[distance - 1], seg_recv.at[distance - 1], me + distance
+        )
+
+    def seg_back():
+        return remote(segwin.at[2], segwin.at[1], seg_send.at[2], seg_recv.at[2], me - 1)
+
+    def own_out(which, head):
+        return remote(
+            (k_ref, v_ref)[which].at[0, :, columns(head)], win.at[which, head, blocks(2, 4)],
+            own_send.at[which, head], own_recv.at[which, head], me + 1,
+        )
+
+    def own_back(which, head):
+        return remote(
+            (k_ref, v_ref)[which].at[0, :, columns(head)], win.at[which, head, blocks(6, 8)],
+            back_send.at[which, head], back_recv.at[which, head], me - 1,
+        )
+
+    def help_out(head):
+        at = pl.ds(head * group * HD, group * HD)
+        return remote(q_ref.at[0, :, at], q_next.at[:, at], help_send.at[head], help_recv.at[head], me - 1)
+
+    def give_out(head):
+        width = group * HD
+        at = pl.ds(head * width if isinstance(head, int) else pl.multiple_of(head * width, width), width)
+        return remote(next_out.at[:, at], out_ref.at[0, :, at], give_send.at[head], give_recv.at[head], me + 1)
+
+    def near_out(which, head):
+        return remote(
+            (k_ref, v_ref)[which].at[0, blocks(1, 2), columns(head)], win.at[which, head, blocks(3, 4)],
+            near_send.at[which, head], near_recv.at[which, head], me + 1,
+        )
+
+    def near_on(which, head):
+        return remote(
+            win.at[which, head, blocks(3, 4)], win.at[which, head, blocks(1, 2)],
+            near_send.at[which, head], near_recv.at[which, head], me + 1,
+        )
+
+    def spot(piece, base):
+        at = pl.multiple_of((base - piece // (2 * HK)) * LANES, LANES)
+        return (piece % 2, (piece % (2 * HK)) // 2, pl.ds(at, LANES))
+
+    def mix_out(piece):
+        return remote(mix.at[piece], win.at[spot(piece, 2)], mix_send.at[piece], mix_recv.at[piece], me + 1)
+
+    def mix_on(which, head):
+        piece = 2 * head + which
+        return remote(
+            win.at[which, head, blocks(2, 3)], win.at[which, head, blocks(0, 1)],
+            mix_send.at[piece], mix_recv.at[piece], me + 1,
+        )
+
+    def lse_copy(pair):
+        return remote(lse_out.at[pair], lse_in.at[pair], lse_send.at[pair], lse_recv.at[pair], me + 1)
+
+    def q_back(which):
+        return remote(
+            q_ref.at[0, blocks(0, 1), columns(which)], q_in.at[which], q_send.at[which], q_recv.at[which], me - 1
+        )
+
+    freq = frequencies()
+    lane = lax.broadcasted_iota(jnp.int32, (LANES, LANES), 1)
+    row = lax.broadcasted_iota(jnp.int32, (LANES, LANES), 0)
+    sign = jnp.where(lane < HD // 2, F32(-1.0), F32(1.0))
+    ones = jnp.ones((LANES, LANES), BF16)
+
+    def start_of(index, pieces):
+        column = jnp.broadcast_to(segwin[index].astype(F32), (LANES, rows)).T
+        smaller = jnp.zeros((rows, LANES), F32)
+        for piece in pieces:
+            smaller = smaller + jnp.where(piece < column, F32(1.0), F32(0.0))
+        return jnp.dot(smaller.astype(BF16), ones, preferred_element_type=F32)
+
+    def tables(start, block):
+        sine, cosine = sin_cos(((row + block * LANES).astype(F32) - start) * freq)
+        at = blocks(block, block + 1)
+        sines[at] = sine * sign
+        cosines[at] = cosine
+
+    def masks(where, start, tile, low, own):
+        first = start.T
+        last = (lane + (own + tile) * LANES).astype(F32)
+        for block in range(low, own + 1 + tile):
+            key = (row + block * LANES).astype(F32)
+            live = key >= first
+            if block == own + tile:
+                live = live & (key <= last)
+            where[tile, blocks(block, block + 1)] = jnp.where(live, F32(0.0), F32(MASKED))
+
+    def turn_key(head, block):
+        at = blocks(block, block + 1)
+        krot[head, at] = turned(win[0, head, at], cosines[at], sines[at])
+        vturn[head, 0:HD, at] = win[1, head, at].T
+
+    def turn_queries(head, source, target, own):
+        for tile in range(2):
+            place = blocks(own + tile, own + 1 + tile)
+            cosine, sine = cosines[place], sines[place]
+            for member in range(group):
+                target[head, tile, blocks(member, member + 1)] = turned(
+                    source[blocks(tile, tile + 1), columns(head * group + member)], cosine, sine
+                )
+
+    def raw_scores(keys, one):
+        return lax.dot_general(keys, one, (((1,), (1,)), ((), ())), preferred_element_type=F32)
+
+    def spread(part):
+        return jnp.concatenate([part] * group, axis=1)
+
+    def scores_of(head, tile, first, last):
+        at = blocks(first, last)
+        return raw_scores(krot[head, at], qrot[head, tile]) + spread(bias[tile, at])
+
+    def summed(head, weight, at):
+        return jnp.dot(vturn[head, :, at], weight.astype(BF16), preferred_element_type=F32)
+
+    def keep(head, tile, top, both):
+        tops[head, tile] = jnp.broadcast_to(top, tops.shape[2:])
+        totals[head, tile] = both
+
+    def put(head, tile, total, under, target=None):
+        value = (total * (1.0 / under)).astype(BF16)
+        for member in range(group):
+            done = value[:, member * LANES:(member + 1) * LANES].T
+            if target is None:
+                out_ref[0, blocks(tile, tile + 1), columns(head * group + member)] = done
+            else:
+                target[blocks(tile, tile + 1), columns(head * group + member)] = done
+
+    def fresh(head, first, last=5, ones=qrot, mask=bias):
+        found = []
+        for tile in range(2):
+            at = blocks(first, last + tile)
+            found.append(raw_scores(krot[head, at], ones[head, tile]) + spread(mask[tile, at]))
+        result = []
+        for tile in range(2):
+            top = jnp.max(found[tile], axis=0, keepdims=True)
+            weight = jnp.exp2((found[tile] - top) * scale)
+            result.append((top, summed(head, weight, blocks(first, last + tile))))
+        return result
+
+    def more(head, tile, scores, first, last, extra=None):
+        old = tops[head, tile, 0:1]
+        top = jnp.maximum(old, jnp.max(scores, axis=0, keepdims=True))
+        if extra is not None:
+            top = jnp.maximum(top, extra)
+        ratio = jnp.exp2((old - top) * scale)
+        weight = jnp.exp2((scores - top) * scale)
+        return top, totals[head, tile] * ratio + summed(head, weight, blocks(first, last))
+
+    seg_copy.wait()
+    for distance in (1, 2):
+        @pl.when(me + distance < count)
+        def _():
+            seg_out(distance).start()
+
+    @pl.when(me == 1)
+    def _():
+        seg_back().start()
+
+    @pl.when(me == 2)
+    def _():
+        for which in range(heads):
+            q_back(which).start()
+
+    @pl.when(me == 1)
+    def _():
+        for which, head in every:
+            near_out(which, head).start()
+        for which, head in every[:-2]:
+            own_back(which, head).start()
+        for head in range(HK - 1):
+            help_out(head).start()
+
+    @pl.when(me % 2 == 0)
+    def _():
+        for which, head in every:
+            own_out(which, head).start()
+
+    for tile in (1, 0):
+        for which, head in every:
+            own_copies[which, head, tile].start()
+
+    @pl.when(me == 1)
+    def _():
+        keep_copy.start()
+
+    @pl.when(me != 1)
+    def _():
+        for tile in range(2):
+            q_copies[tile].start()
+
+    @pl.when(me <= 1)
+    def _():
+        segwin[0] = jnp.full((1, rows), -1, jnp.int32)
+
+    @pl.when(me == 0)
+    def _():
+        seg_back().wait_recv()
+
+    for distance in (1, 2):
+        @pl.when(me >= distance)
+        def _():
+            seg_out(distance).wait_recv()
+
+    for which, head in every:
+        for tile in range(2):
+            own_copies[which, head, tile].wait()
+
+    pieces = []
+    for index in range(3):
+        seg_row = segwin[index].astype(F32)
+        pieces += [seg_row[:, at:at + LANES] for at in range(0, rows, LANES)]
+    shift = jnp.where(me == 0, rows, 0).astype(F32)
+    begin = start_of(2, pieces) + shift
+    start = start_of(1, pieces) + shift
+    vturn[:, HD:] = jnp.ones((HK, vturn.shape[1] - HD, vturn.shape[2]), BF16)
+    tables(begin[:LANES], 4)
+    for tile in range(2):
+        tables(start[tile * LANES:(tile + 1) * LANES], jnp.where(me == 0, 6, 2) + tile)
+
+    @pl.when(me == 1)
+    def _():
+        late = begin[rows - 1:rows]
+        sine, cosine = sin_cos(((row + 6 * LANES).astype(F32) - late) * freq)
+        q_sine[...] = sine * sign
+        q_cosine[...] = cosine
+        for block in range(3):
+            key = (row + (2 + block) * LANES).astype(F32)
+            q_bias[blocks(block, block + 1)] = jnp.where(key >= late, F32(0.0), F32(MASKED))
+        given = late < F32(3 * LANES)
+        seen = blocks(2, 5)
+        for head in range(HK):
+            turn_key(head, 4)
+        for which, head in every:
+            own_out(which, head).wait_recv()
+
+        @pl.loop(0, HK)
+        def _(head):
+            turn_key(head, 2)
+            turn_key(head, 3)
+            for pair in range(group // 2):
+                twin = [head * group + 2 * pair + member for member in range(2)]
+                for which in twin:
+                    q_back(which).wait_recv()
+                one = jnp.concatenate([turned(q_in[which], q_cosine[...], q_sine[...]) for which in twin], axis=0)
+                scores = raw_scores(krot[head, seen], one) + jnp.concatenate([q_bias[...]] * 2, axis=1)
+                top = jnp.max(scores, axis=0, keepdims=True)
+                both = summed(head, jnp.exp2((scores - top) * scale), seen)
+                under = both[HD:HD + 1]
+                total = both[:HD] * (1.0 / under)
+                for member, which in enumerate(twin):
+                    mix[which] = jnp.where(
+                        given, total[:, member * LANES:(member + 1) * LANES], win[spot(which, 4)].astype(F32)
+                    ).astype(BF16)
+                lse = top + jnp.log(under) * F32(math.sqrt(HD))
+                for member in range(2):
+                    lse_out[2 * head + pair, member:member + 1] = lse[:, member * LANES:(member + 1) * LANES]
+                for which in twin:
+                    mix_out(which).start()
+                lse_copy(2 * head + pair).start()
+
+    tables(begin[LANES:], 5)
+    mark[...] = begin[:LANES].T[:8]
+    first = jnp.where((begin < F32(LANES)) & (me == 2), F32(3 * LANES), begin)
+    for tile in range(2):
+        masks(bias, first[tile * LANES:(tile + 1) * LANES], tile, 0, 4)
+
+    @pl.when(me == 1)
+    def _():
+        keep_copy.wait()
+        head = HK - 1
+        turn_queries(head, q_own, qrot, 4)
+        turn_key(head, 5)
+        for tile, (top, both) in enumerate(fresh(head, 2)):
+            put(head, tile, both[:HD], both[HD:HD + 1])
+
+    @pl.when(me == 0)
+    def _():
+        for tile in range(2):
+            masks(next_bias, start[tile * LANES:(tile + 1) * LANES], tile, 4, 6)
+            q_copies[tile].wait()
+
+        @pl.loop(0, HK)
+        def _(head):
+            turn_queries(head, q_own, qrot, 4)
+            for block in (4, 5):
+                turn_key(head, block)
+            for tile, (top, both) in enumerate(fresh(head, 4)):
+                put(head, tile, both[:HD], both[HD:HD + 1])
+
+        for which, head in every[:-2]:
+            own_back(which, head).wait_recv()
+        for head in range(HK - 1):
+            help_out(head).wait_recv()
+
+        @pl.loop(0, HK - 1)
+        def _(head):
+            turn_queries(head, q_next, next_rot, 6)
+            for block in (6, 7):
+                turn_key(head, block)
+            for tile, (top, both) in enumerate(fresh(head, 4, 7, next_rot, next_bias)):
+                put(head, tile, both[:HD], both[HD:HD + 1], next_out)
+            give_out(head).start()
+
+    @pl.when(me >= 2)
+    def _():
+        start = start_of(0, pieces)
+        for tile in range(2):
+            tables(start[tile * LANES:(tile + 1) * LANES], tile)
+
+        for tile in range(2):
+            q_copies[tile].wait()
+
+        @pl.loop(0, HK)
+        def _(head):
+            turn_queries(head, q_own, qrot, 4)
+            for block in (4, 5):
+                turn_key(head, block)
+
+    @pl.when(me == 2)
+    def _():
+        @pl.loop(0, HK)
+        def _(head):
+            for which in range(2):
+                near_out(which, head).wait_recv()
+                near_on(which, head).start()
+            turn_key(head, 3)
+            for tile, (top, both) in enumerate(fresh(head, 3)):
+                keep(head, tile, top, both)
+
+        @pl.loop(0, HK)
+        def _(head):
+            for which in range(2):
+                mix_out(2 * head + which).wait_recv()
+                mix_on(which, head).start()
+            turn_key(head, 2)
+            found = [scores_of(head, tile, 2, 3) for tile in range(2)]
+            for tile in range(2):
+                keep(head, tile, *more(head, tile, found[tile], 2, 3))
+
+        @pl.loop(0, HK)
+        def _(head):
+            for which in range(2):
+                mix_out(2 * HK + 2 * head + which).wait_recv()
+                lse_copy(2 * head + which).wait_recv()
+            turn_key(head, 1)
+            found = [scores_of(head, tile, 1, 2) for tile in range(2)]
+            crossing = spread(mark[0:1] < F32(LANES))
+            lse = jnp.concatenate(
+                [lse_in[2 * head + member // 2, member % 2:member % 2 + 1] for member in range(group)], axis=1
+            )
+            lse = jnp.where(crossing, lse, F32(MASKED))
+            top, both = more(head, 0, found[0], 1, 2, lse)
+            share = jnp.exp2((lse - top) * scale)
+            given = jnp.concatenate([win[spot(head * group + member, 2)] for member in range(group)], axis=1)
+            put(head, 0, both[:HD] + given.astype(F32) * share, both[HD:HD + 1] + share)
+            top, both = more(head, 1, found[1], 1, 2)
+            put(head, 1, both[:HD], both[HD:HD + 1])
+
+    @pl.when(me == 3)
+    def _():
+        @pl.loop(0, HK)
+        def _(head):
+            for which in range(2):
+                own_out(which, head).wait_recv()
+            for block in (2, 3):
+                turn_key(head, block)
+            for tile, (top, both) in enumerate(fresh(head, 2)):
+                keep(head, tile, top, both)
+
+        @pl.loop(0, HK)
+        def _(head):
+            for which in range(2):
+                near_on(which, head).wait_recv()
+                mix_on(which, head).wait_recv()
+            for block in range(2):
+                turn_key(head, block)
+            found = [scores_of(head, tile, tile, 2) for tile in range(2)]
+            for tile in range(2):
+                top, both = more(head, tile, found[tile], tile, 2)
+                put(head, tile, both[:HD], both[HD:HD + 1])
+
+    for distance in (1, 2):
+        @pl.when(me + distance < count)
+        def _():
+            seg_out(distance).wait_send()
+
+    @pl.when(me % 2 == 0)
+    def _():
+        for which, head in every:
+            own_out(which, head).wait_send()
+
+    @pl.when(me == 0)
+    def _():
+        for head in range(HK - 1):
+            give_out(head).wait_send()
+
+    @pl.when(me == 1)
+    def _():
+        @pl.loop(0, 2 * HK)
+        def _(pair):
+            for member in range(2):
+                mix_out(2 * pair + member).wait_send()
+            lse_copy(pair).wait_send()
+
+        for head in range(HK - 1):
+            help_out(head).wait_send()
+            give_out(head).wait_recv()
+        seg_back().wait_send()
+        for which, head in every:
+            near_out(which, head).wait_send()
+            if head < HK - 1:
+                own_back(which, head).wait_send()
+
+    @pl.when(me == 2)
+    def _():
+        for which, head in every:
+            near_on(which, head).wait_send()
+            mix_on(which, head).wait_send()
+
+        @pl.loop(0, heads)
+        def _(which):
+            q_back(which).wait_send()
+
+
+def relay(queries, keys, values, segments):
+    rows = queries.shape[1]
+    heads = queries.shape[2] // HD
+    width = 3 * rows
+    stack = heads // HK * LANES
+    anywhere = pl.BlockSpec(memory_space=pltpu.HBM)
+    dma = pltpu.SemaphoreType.DMA
+    both = dma((2, HK))
+    return pl.pallas_call(
+        relay_kernel,
+        out_shape=pltpu.VMEM(queries.shape, BF16),
+        in_specs=[anywhere] * 4,
+        out_specs=pl.BlockSpec(memory_space=pltpu.VMEM),
+        scratch_shapes=[
+            pltpu.VMEM((rows, heads * HD), BF16),
+            pltpu.VMEM((2, HK, width + rows, HD), BF16),
+            pltpu.VMEM((3, 1, rows), jnp.int32),
+            pltpu.VMEM((HK, width + rows, HD), BF16),
+            pltpu.VMEM((HK, HD + 16, width + rows), BF16),
+            pltpu.VMEM((HK, 2, stack, HD), BF16),
+            pltpu.VMEM((HK, 2, 8, stack), F32),
+            pltpu.VMEM((HK, 2, HD + 16, stack), F32),
+            pltpu.VMEM((width + rows, HD), F32),
+            pltpu.VMEM((width + rows, HD), F32),
+            pltpu.VMEM((2, width, LANES), F32),
+            pltpu.VMEM((heads, LANES, HD), BF16),
+            pltpu.VMEM((heads, LANES, HD), BF16),
+            pltpu.VMEM((heads // 2, 8, LANES), F32),
+            pltpu.VMEM((heads // 2, 8, LANES), F32),
+            pltpu.VMEM((LANES, HD), F32),
+            pltpu.VMEM((LANES, HD), F32),
+            pltpu.VMEM((3 * LANES, LANES), F32),
+            pltpu.VMEM((8, LANES), F32),
+            pltpu.VMEM((rows, heads * HD), BF16),
+            pltpu.VMEM((HK, 2, stack, HD), BF16),
+            pltpu.VMEM((2, width + rows, LANES), F32),
+            pltpu.VMEM((rows, heads * HD), BF16),
+            dma((2,)), dma, dma((2, HK, 2)), dma((3,)), dma((3,)), both, both, both, both,
+            both, both, dma((heads,)), dma((heads,)), dma((heads // 2,)), dma((heads // 2,)),
+            dma((heads,)), dma((heads,)), dma((HK,)), dma((HK,)), dma((HK,)), dma((HK,)),
+        ],
+        compiler_params=pltpu.CompilerParams(
+            collective_id=0, has_side_effects=True, vmem_limit_bytes=60 * 1024 * 1024
+        ),
+        name="attend",
+    )(queries, keys, values, segments)
+
+
 def body(queries, keys, values, segments):
     count = lax.axis_size("ctx")
     hops = count // 2
@@ -277,7 +816,8 @@
     width = (hops + 1) * rows
     span = hops * rows + LANES
     heads = queries.shape[2] // HD
-    group = heads // HK
+    if count == 4 and rows == 2 * LANES and heads == 4 * HK:
+        return relay(queries, keys, values, segments)
     anywhere = pl.BlockSpec(memory_space=pltpu.HBM)
     dma = pltpu.SemaphoreType.DMA
     return pl.pallas_call(

time: 17.1 us -> 16.3 us (0.953)
  the two profiles are of different devices: /device:TPU:21 before, /device:TPU:28 now
where the time goes in v1:
time: 16.3 us; the launch traced here: 16.1 us
  Pallas kernels  15.1 us (93%)
  local copies, waits for them, and re-layouts  0.97 us (6%)
    pallas_call x1, Pallas kernels, relay(): pl.pallas_call(relay_kernel, out_shape=pltpu.VMEM(queries.shape, BF16), i...  15.1 us
    unnamed x1, local copies, waits for them, and re-layouts  0.97 us

profile of v1, /device:TPU:28, one launch (start us, length us, event | category | flops | bytes accessed | tf_op | source)
XLA Modules:
  0.0 16.1 jit_solution(5298839538305637200)
XLA Ops:
  0.0 15.1 %attend.1 = bf16[1,256,2048]{2,1,0:T(8,128)(2,1)S(1)} custom-call(bf16[1,256,2048]{2,1,0:T(8,128)(2,1)} %q_ref.1, bf16[1,256,512]{2,1,0:T(8,128)(2,1)} %k_ref.1, bf16[1,256,512]{2,1,0:T(8,128)(2,1)} %v_ref.1, s32[1,256]{1,0:T(1,128)} %seg_ref.1), custom_call_target="tpu_custom_call" | custom-call | tf_op jit(solution)/shard_map/attend/pallas_call | solution.py:772
  15.2 1.0 %copy.6 = bf16[1,256,2048]{2,1,0:T(8,128)(2,1)} copy(bf16[1,256,2048]{2,1,0:T(8,128)(2,1)S(1)} %attend.1) | data formatting | bytes 2097152

commit v2 on v1

--- a/solution.py
+++ b/solution.py
@@ -273,7 +273,7 @@
 def relay_kernel(
     q_ref, k_ref, v_ref, seg_ref, out_ref,
     q_own, win, segwin, krot, vturn, qrot, tops, totals, sines, cosines, bias,
-    q_in, mix, lse_out, lse_in, q_sine, q_cosine, q_bias, mark, q_next, next_rot, next_bias, next_out,
+    q_in, mix, mixed, lse_out, lse_in, q_sine, q_cosine, q_bias, mark, q_next, next_rot, next_bias, next_out,
     q_sem, seg_sem, own_sem, seg_send, seg_recv, back_send, back_recv, own_send, own_recv,
     near_send, near_recv, mix_send, mix_recv, lse_send, lse_recv, q_send, q_recv,
     help_send, help_recv, give_send, give_recv,
@@ -281,7 +281,7 @@
     me = lax.axis_index("ctx")
     count = lax.axis_size("ctx")
     rows = q_own.shape[0]
-    heads = q_in.shape[0]
+    heads = q_own.shape[1] // HD
     group = heads // HK
     scale = F32(math.log2(math.e) / math.sqrt(HD))
 
@@ -293,24 +293,19 @@
     def columns(head):
         return pl.ds(head * HD if isinstance(head, int) else pl.multiple_of(head * HD, HD), HD)
 
-    every = [(which, head) for head in range(HK) for which in range(2)]
-    own_copies = {
-        (which, head, tile): pltpu.make_async_copy(
-            (k_ref, v_ref)[which].at[0, blocks(tile, tile + 1), columns(head)],
-            win.at[which, head, blocks(4 + tile, 5 + tile)], own_sem.at[which, head, tile],
-        )
-        for which, head in every
-        for tile in range(2)
-    }
+    def duo(pair):
+        at = pair * 2 * HD
+        return pl.ds(at if isinstance(pair, int) else pl.multiple_of(at, 2 * HD), 2 * HD)
+
+    sources = (k_ref, v_ref)
+    own, before, after = blocks(4, 6), blocks(2, 4), blocks(6, 8)
+    own_copies = [
+        pltpu.make_async_copy(sources[which].at[0], win.at[which, own], own_sem.at[which]) for which in range(2)
+    ]
     seg_copy = pltpu.make_async_copy(seg_ref, segwin.at[2], seg_sem)
-    q_copies = [
-        pltpu.make_async_copy(
-            q_ref.at[0, blocks(tile, tile + 1)], q_own.at[blocks(tile, tile + 1)], q_sem.at[tile]
-        )
-        for tile in range(2)
-    ]
+    q_copy = pltpu.make_async_copy(q_ref.at[0], q_own, q_sem)
     tail = pl.ds((HK - 1) * group * HD, group * HD)
-    keep_copy = pltpu.make_async_copy(q_ref.at[0, :, tail], q_own.at[:, tail], q_sem.at[0])
+    keep_copy = pltpu.make_async_copy(q_ref.at[0, :, tail], q_own.at[:, tail], q_sem)
     seg_copy.start()
 
     barrier = pltpu.get_barrier_semaphore()
@@ -340,60 +335,52 @@
     def seg_back():
         return remote(segwin.at[2], segwin.at[1], seg_send.at[2], seg_recv.at[2], me - 1)
 
-    def own_out(which, head):
-        return remote(
-            (k_ref, v_ref)[which].at[0, :, columns(head)], win.at[which, head, blocks(2, 4)],
-            own_send.at[which, head], own_recv.at[which, head], me + 1,
-        )
-
-    def own_back(which, head):
-        return remote(
-            (k_ref, v_ref)[which].at[0, :, columns(head)], win.at[which, head, blocks(6, 8)],
-            back_send.at[which, head], back_recv.at[which, head], me - 1,
-        )
-
-    def help_out(head):
-        at = pl.ds(head * group * HD, group * HD)
-        return remote(q_ref.at[0, :, at], q_next.at[:, at], help_send.at[head], help_recv.at[head], me - 1)
+    def own_out(which):
+        return remote(sources[which].at[0], win.at[which, before], own_send, own_recv.at[which], me + 1)
+
+    def own_back(which):
+        return remote(sources[which].at[0], win.at[which, after], back_send, back_recv.at[which], me - 1)
+
+    helped = pl.ds(0, (HK - 1) * group * HD)
+
+    def help_out():
+        return remote(q_ref.at[0, :, helped], q_next.at[:, helped], help_send, help_recv, me - 1)
 
     def give_out(head):
         width = group * HD
         at = pl.ds(head * width if isinstance(head, int) else pl.multiple_of(head * width, width), width)
-        return remote(next_out.at[:, at], out_ref.at[0, :, at], give_send.at[head], give_recv.at[head], me + 1)
-
-    def near_out(which, head):
+        return remote(next_out.at[:, at], out_ref.at[0, :, at], give_send, give_recv.at[head], me + 1)
+
+    quarters = [(which, part) for part in range(2) for which in range(2)]
+
+    def near_out(which, part):
         return remote(
-            (k_ref, v_ref)[which].at[0, blocks(1, 2), columns(head)], win.at[which, head, blocks(3, 4)],
-            near_send.at[which, head], near_recv.at[which, head], me + 1,
+            sources[which].at[0, blocks(1, 2), duo(part)], win.at[which, blocks(3, 4), duo(part)],
+            near_send, near_recv.at[which, part], me + 1,
         )
 
-    def near_on(which, head):
+    def near_on(which, part):
         return remote(
-            win.at[which, head, blocks(3, 4)], win.at[which, head, blocks(1, 2)],
-            near_send.at[which, head], near_recv.at[which, head], me + 1,
+            win.at[which, blocks(3, 4), duo(part)], win.at[which, blocks(1, 2), duo(part)],
+            near_send, near_recv.at[which, part], me + 1,
         )
 
-    def spot(piece, base):
-        at = pl.multiple_of((base - piece // (2 * HK)) * LANES, LANES)
-        return (piece % 2, (piece % (2 * HK)) // 2, pl.ds(at, LANES))
-
-    def mix_out(piece):
-        return remote(mix.at[piece], win.at[spot(piece, 2)], mix_send.at[piece], mix_recv.at[piece], me + 1)
-
-    def mix_on(which, head):
-        piece = 2 * head + which
-        return remote(
-            win.at[which, head, blocks(2, 3)], win.at[which, head, blocks(0, 1)],
-            mix_send.at[piece], mix_recv.at[piece], me + 1,
-        )
-
-    def lse_copy(pair):
-        return remote(lse_out.at[pair], lse_in.at[pair], lse_send.at[pair], lse_recv.at[pair], me + 1)
-
-    def q_back(which):
-        return remote(
-            q_ref.at[0, blocks(0, 1), columns(which)], q_in.at[which], q_send.at[which], q_recv.at[which], me - 1
-        )
+    def mix_out(pair):
+        return remote(mix.at[pair], mixed.at[pair], mix_send, mix_recv.at[pair], me + 1)
+
+    def mix_on(head):
+        return remote(mixed.at[head], mixed.at[head], mix_send, mix_recv.at[head], me + 1)
+
+    few = pl.ds(0, group)
+
+    def lse_copy(head):
+        return remote(lse_out.at[head, few], lse_in.at[head, few], lse_send, lse_recv.at[head], me + 1)
+
+    def q_back(pair):
+        return remote(q_ref.at[0, blocks(0, 1), duo(pair)], q_in.at[pair], q_send, q_recv.at[pair], me - 1)
+
+    def all_sent(ref, sent, received):
+        remote(ref, ref, sent, received, me + 1).wait_send()
 
     freq = frequencies()
     lane = lax.broadcasted_iota(jnp.int32, (LANES, LANES), 1)
@@ -424,10 +411,14 @@
                 live = live & (key <= last)
             where[tile, blocks(block, block + 1)] = jnp.where(live, F32(0.0), F32(MASKED))
 
+    def turn(head, block, keys, values):
+        at = blocks(block, block + 1)
+        krot[head, at] = turned(keys, cosines[at], sines[at])
+        vturn[head, 0:HD, at] = values.T
+
     def turn_key(head, block):
         at = blocks(block, block + 1)
-        krot[head, at] = turned(win[0, head, at], cosines[at], sines[at])
-        vturn[head, 0:HD, at] = win[1, head, at].T
+        turn(head, block, win[0, at, columns(head)], win[1, at, columns(head)])
 
     def turn_queries(head, source, target, own):
         for tile in range(2):
@@ -497,26 +488,24 @@
 
     @pl.when(me == 2)
     def _():
-        for which in range(heads):
-            q_back(which).start()
+        for pair in range(heads // 2):
+            q_back(pair).start()
 
     @pl.when(me == 1)
     def _():
-        for which, head in every:
-            near_out(which, head).start()
-        for which, head in every[:-2]:
-            own_back(which, head).start()
-        for head in range(HK - 1):
-            help_out(head).start()
+        for which, part in quarters:
+            near_out(which, part).start()
+        for which in range(2):
+            own_back(which).start()
+        help_out().start()
 
     @pl.when(me % 2 == 0)
     def _():
-        for which, head in every:
-            own_out(which, head).start()
-
-    for tile in (1, 0):
-        for which, head in every:
-            own_copies[which, head, tile].start()
+        for which in range(2):
+            own_out(which).start()
+
+    for which in range(2):
+        own_copies[which].start()
 
     @pl.when(me == 1)
     def _():
@@ -524,8 +513,7 @@
 
     @pl.when(me != 1)
     def _():
-        for tile in range(2):
-            q_copies[tile].start()
+        q_copy.start()
 
     @pl.when(me <= 1)
     def _():
@@ -540,9 +528,8 @@
         def _():
             seg_out(distance).wait_recv()
 
-    for which, head in every:
-        for tile in range(2):
-            own_copies[which, head, tile].wait()
+    for which in range(2):
+        own_copies[which].wait()
 
     pieces = []
     for index in range(3):
@@ -569,33 +556,40 @@
         seen = blocks(2, 5)
         for head in range(HK):
             turn_key(head, 4)
-        for which, head in every:
-            own_out(which, head).wait_recv()
+        for which in range(2):
+            own_out(which).wait_recv()
 
         @pl.loop(0, HK)
         def _(head):
             turn_key(head, 2)
             turn_key(head, 3)
-            for pair in range(group // 2):
-                twin = [head * group + 2 * pair + member for member in range(2)]
-                for which in twin:
-                    q_back(which).wait_recv()
-                one = jnp.concatenate([turned(q_in[which], q_cosine[...], q_sine[...]) for which in twin], axis=0)
+            for part in range(group // 2):
+                pair = 2 * head + part
+                q_back(pair).wait_recv()
+                one = jnp.concatenate(
+                    [
+                        turned(q_in[pair, :, member * HD:(member + 1) * HD], q_cosine[...], q_sine[...])
+                        for member in range(2)
+                    ],
+                    axis=0,
+                )
                 scores = raw_scores(krot[head, seen], one) + jnp.concatenate([q_bias[...]] * 2, axis=1)
                 top = jnp.max(scores, axis=0, keepdims=True)
                 both = summed(head, jnp.exp2((scores - top) * scale), seen)
                 under = both[HD:HD + 1]
                 total = both[:HD] * (1.0 / under)
-                for member, which in enumerate(twin):
-                    mix[which] = jnp.where(
-                        given, total[:, member * LANES:(member + 1) * LANES], win[spot(which, 4)].astype(F32)
+                place = blocks(4 - pair // HK, None)
+                for member in range(2):
+                    mix[pair, member] = jnp.where(
+                        given, total[:, member * LANES:(member + 1) * LANES],
+                        win[member, place, columns(pair % HK)].astype(F32),
                     ).astype(BF16)
                 lse = top + jnp.log(under) * F32(math.sqrt(HD))
                 for member in range(2):
-                    lse_out[2 * head + pair, member:member + 1] = lse[:, member * LANES:(member + 1) * LANES]
-                for which in twin:
-                    mix_out(which).start()
-                lse_copy(2 * head + pair).start()
+                    at = 2 * part + member
+                    lse_out[head, at:at + 1] = lse[:, member * LANES:(member + 1) * LANES]
+                mix_out(pair).start()
+            lse_copy(head).start()
 
     tables(begin[LANES:], 5)
     mark[...] = begin[:LANES].T[:8]
@@ -616,7 +610,7 @@
     def _():
         for tile in range(2):
             masks(next_bias, start[tile * LANES:(tile + 1) * LANES], tile, 4, 6)
-            q_copies[tile].wait()
+        q_copy.wait()
 
         @pl.loop(0, HK)
         def _(head):
@@ -626,10 +620,9 @@
             for tile, (top, both) in enumerate(fresh(head, 4)):
                 put(head, tile, both[:HD], both[HD:HD + 1])
 
-        for which, head in every[:-2]:
-            own_back(which, head).wait_recv()
-        for head in range(HK - 1):
-            help_out(head).wait_recv()
+        for which in range(2):
+            own_back(which).wait_recv()
+        help_out().wait_recv()
 
         @pl.loop(0, HK - 1)
         def _(head):
@@ -646,8 +639,7 @@
         for tile in range(2):
             tables(start[tile * LANES:(tile + 1) * LANES], tile)
 
-        for tile in range(2):
-            q_copies[tile].wait()
+        q_copy.wait()
 
         @pl.loop(0, HK)
         def _(head):
@@ -657,62 +649,63 @@
 
     @pl.when(me == 2)
     def _():
+        for which, part in quarters:
+            near_out(which, part).wait_recv()
+            near_on(which, part).start()
+
         @pl.loop(0, HK)
         def _(head):
-            for which in range(2):
-                near_out(which, head).wait_recv()
-                near_on(which, head).start()
             turn_key(head, 3)
             for tile, (top, both) in enumerate(fresh(head, 3)):
                 keep(head, tile, top, both)
 
         @pl.loop(0, HK)
         def _(head):
-            for which in range(2):
-                mix_out(2 * head + which).wait_recv()
-                mix_on(which, head).start()
-            turn_key(head, 2)
+            mix_out(head).wait_recv()
+            mix_on(head).start()
+            turn(head, 2, mixed[head, 0], mixed[head, 1])
             found = [scores_of(head, tile, 2, 3) for tile in range(2)]
             for tile in range(2):
                 keep(head, tile, *more(head, tile, found[tile], 2, 3))
 
         @pl.loop(0, HK)
         def _(head):
-            for which in range(2):
-                mix_out(2 * HK + 2 * head + which).wait_recv()
-                lse_copy(2 * head + which).wait_recv()
-            turn_key(head, 1)
+            mix_out(HK + head).wait_recv()
+            lse_copy(head).wait_recv()
+            turn(head, 1, mixed[HK + head, 0], mixed[HK + head, 1])
             found = [scores_of(head, tile, 1, 2) for tile in range(2)]
             crossing = spread(mark[0:1] < F32(LANES))
-            lse = jnp.concatenate(
-                [lse_in[2 * head + member // 2, member % 2:member % 2 + 1] for member in range(group)], axis=1
-            )
+            lse = jnp.concatenate([lse_in[head, member:member + 1] for member in range(group)], axis=1)
             lse = jnp.where(crossing, lse, F32(MASKED))
             top, both = more(head, 0, found[0], 1, 2, lse)
             share = jnp.exp2((lse - top) * scale)
-            given = jnp.concatenate([win[spot(head * group + member, 2)] for member in range(group)], axis=1)
+            given = jnp.concatenate(
+                [mixed[2 * head + member // 2, member % 2] for member in range(group)], axis=1
+            )
             put(head, 0, both[:HD] + given.astype(F32) * share, both[HD:HD + 1] + share)
             top, both = more(head, 1, found[1], 1, 2)
             put(head, 1, both[:HD], both[HD:HD + 1])
 
     @pl.when(me == 3)
     def _():
+        for which in range(2):
+            own_out(which).wait_recv()
+
         @pl.loop(0, HK)
         def _(head):
-            for which in range(2):
-                own_out(which, head).wait_recv()
             for block in (2, 3):
                 turn_key(head, block)
             for tile, (top, both) in enumerate(fresh(head, 2)):
                 keep(head, tile, top, both)
 
+        for which, part in quarters:
+            near_on(which, part).wait_recv()
+
         @pl.loop(0, HK)
         def _(head):
-            for which in range(2):
-                near_on(which, head).wait_recv()
-                mix_on(which, head).wait_recv()
-            for block in range(2):
-                turn_key(head, block)
+            mix_on(head).wait_recv()
+            turn(head, 0, mixed[head, 0], mixed[head, 1])
+            turn_key(head, 1)
             found = [scores_of(head, tile, tile, 2) for tile in range(2)]
             for tile in range(2):
                 top, both = more(head, tile, found[tile], tile, 2)
@@ -725,40 +718,28 @@
 
     @pl.when(me % 2 == 0)
     def _():
-        for which, head in every:
-            own_out(which, head).wait_send()
+        all_sent(win.at[:, own], own_send, own_recv.at[0])
 
     @pl.when(me == 0)
     def _():
+        all_sent(next_out.at[:, helped], give_send, give_recv.at[0])
+
+    @pl.when(me == 1)
+    def _():
+        seg_back().wait_send()
+        all_sent(win.at[:, blocks(3, 4)], near_send, near_recv.at[0, 0])
+        all_sent(win.at[:, own], back_send, back_recv.at[0])
+        help_out().wait_send()
+        all_sent(mix, mix_send, mix_recv.at[0])
+        all_sent(lse_out.at[:, few], lse_send, lse_recv.at[0])
         for head in range(HK - 1):
-            give_out(head).wait_send()
-
-    @pl.when(me == 1)
-    def _():
-        @pl.loop(0, 2 * HK)
-        def _(pair):
-            for member in range(2):
-                mix_out(2 * pair + member).wait_send()
-            lse_copy(pair).wait_send()
-
-        for head in range(HK - 1):
-            help_out(head).wait_send()
             give_out(head).wait_recv()
-        seg_back().wait_send()
-        for which, head in every:
-            near_out(which, head).wait_send()
-            if head < HK - 1:
-                own_back(which, head).wait_send()
 
     @pl.when(me == 2)
     def _():
-        for which, head in every:
-            near_on(which, head).wait_send()
-            mix_on(which, head).wait_send()
-
-        @pl.loop(0, heads)
-        def _(which):
-            q_back(which).wait_send()
+        all_sent(win.at[:, blocks(3, 4)], near_send, near_recv.at[0, 0])
+        all_sent(mixed.at[pl.ds(0, HK)], mix_send, mix_recv.at[0])
+        all_sent(q_own.at[blocks(0, 1)], q_send, q_recv.at[0])
 
 
 def relay(queries, keys, values, segments):
@@ -768,7 +749,6 @@
     stack = heads // HK * LANES
     anywhere = pl.BlockSpec(memory_space=pltpu.HBM)
     dma = pltpu.SemaphoreType.DMA
-    both = dma((2, HK))
     return pl.pallas_call(
         relay_kernel,
         out_shape=pltpu.VMEM(queries.shape, BF16),
@@ -776,7 +756,7 @@
         out_specs=pl.BlockSpec(memory_space=pltpu.VMEM),
         scratch_shapes=[
             pltpu.VMEM((rows, heads * HD), BF16),
-            pltpu.VMEM((2, HK, width + rows, HD), BF16),
+            pltpu.VMEM((2, width + rows, HK * HD), BF16),
             pltpu.VMEM((3, 1, rows), jnp.int32),
             pltpu.VMEM((HK, width + rows, HD), BF16),
             pltpu.VMEM((HK, HD + 16, width + rows), BF16),
@@ -786,10 +766,11 @@
             pltpu.VMEM((width + rows, HD), F32),
             pltpu.VMEM((width + rows, HD), F32),
             pltpu.VMEM((2, width, LANES), F32),
-            pltpu.VMEM((heads, LANES, HD), BF16),
-            pltpu.VMEM((heads, LANES, HD), BF16),
-            pltpu.VMEM((heads // 2, 8, LANES), F32),
-            pltpu.VMEM((heads // 2, 8, LANES), F32),
+            pltpu.VMEM((heads // 2, LANES, 2 * HD), BF16),
+            pltpu.VMEM((heads // 2, 2, LANES, HD), BF16),
+            pltpu.VMEM((heads // 2, 2, LANES, HD), BF16),
+            pltpu.VMEM((HK, 8, LANES), F32),
+            pltpu.VMEM((HK, 8, LANES), F32),
             pltpu.VMEM((LANES, HD), F32),
             pltpu.VMEM((LANES, HD), F32),
             pltpu.VMEM((3 * LANES, LANES), F32),
@@ -798,9 +779,9 @@
             pltpu.VMEM((HK, 2, stack, HD), BF16),
             pltpu.VMEM((2, width + rows, LANES), F32),
             pltpu.VMEM((rows, heads * HD), BF16),
-            dma((2,)), dma, dma((2, HK, 2)), dma((3,)), dma((3,)), both, both, both, both,
-            both, both, dma((heads,)), dma((heads,)), dma((heads // 2,)), dma((heads // 2,)),
-            dma((heads,)), dma((heads,)), dma((HK,)), dma((HK,)), dma((HK,)), dma((HK,)),
+            dma, dma, dma((2,)), dma((3,)), dma((3,)), dma, dma((2,)), dma, dma((2,)),
+            dma, dma((2, 2)), dma, dma((heads // 2,)), dma, dma((HK,)), dma, dma((heads // 2,)),
+            dma, dma, dma, dma((HK - 1,)),
         ],
         compiler_params=pltpu.CompilerParams(
             collective_id=0, has_side_effects=True, vmem_limit_bytes=60 * 1024 * 1024

time: 16.3 us -> 15.5 us (0.951)
  Pallas kernels: 15.1 us -> 14.4 us
    pallas_call x1, Pallas kernels: 15.1 us -> 14.4 us  [relay(): pl.pallas_call(relay_kernel, out_shape=pltpu.VMEM(queries.shape, BF16), i...]
where the time goes in v2:
time: 15.5 us; the launch traced here: 15.4 us
  Pallas kernels  14.4 us (93%)
  local copies, waits for them, and re-layouts  0.97 us (6%)
    pallas_call x1, Pallas kernels, relay(): pl.pallas_call(relay_kernel, out_shape=pltpu.VMEM(queries.shape, BF16), i...  14.4 us
    unnamed x1, local copies, waits for them, and re-layouts  0.97 us

profile of v2, /device:TPU:28, one launch (start us, length us, event | category | flops | bytes accessed | tf_op | source)
XLA Modules:
  0.0 15.4 jit_solution(16787070545993413000)
XLA Ops:
  0.0 14.4 %attend.1 = bf16[1,256,2048]{2,1,0:T(8,128)(2,1)S(1)} custom-call(bf16[1,256,2048]{2,1,0:T(8,128)(2,1)} %q_ref.1, bf16[1,256,512]{2,1,0:T(8,128)(2,1)} %k_ref.1, bf16[1,256,512]{2,1,0:T(8,128)(2,1)} %v_ref.1, s32[1,256]{1,0:T(1,128)} %seg_ref.1), custom_call_target="tpu_custom_call" | custom-call | tf_op jit(solution)/shard_map/attend/pallas_call | solution.py:752
  14.4 1.0 %copy.6 = bf16[1,256,2048]{2,1,0:T(8,128)(2,1)} copy(bf16[1,256,2048]{2,1,0:T(8,128)(2,1)S(1)} %attend.1) | data formatting | bytes 2097152

commit v3 on v2

--- a/solution.py
+++ b/solution.py
@@ -456,15 +456,16 @@
                 target[blocks(tile, tile + 1), columns(head * group + member)] = done
 
     def fresh(head, first, last=5, ones=qrot, mask=bias):
+        units = [(one, tile) for one in (head if isinstance(head, list) else [head]) for tile in range(2)]
         found = []
-        for tile in range(2):
+        for one, tile in units:
             at = blocks(first, last + tile)
-            found.append(raw_scores(krot[head, at], ones[head, tile]) + spread(mask[tile, at]))
+            found.append(raw_scores(krot[one, at], ones[one, tile]) + spread(mask[tile, at]))
         result = []
-        for tile in range(2):
-            top = jnp.max(found[tile], axis=0, keepdims=True)
-            weight = jnp.exp2((found[tile] - top) * scale)
-            result.append((top, summed(head, weight, blocks(first, last + tile))))
+        for (one, tile), scores in zip(units, found):
+            top = jnp.max(scores, axis=0, keepdims=True)
+            weight = jnp.exp2((scores - top) * scale)
+            result.append((top, summed(one, weight, blocks(first, last + tile))))
         return result
 
     def more(head, tile, scores, first, last, extra=None):
@@ -636,8 +637,11 @@
     @pl.when(me >= 2)
     def _():
         start = start_of(0, pieces)
-        for tile in range(2):
-            tables(start[tile * LANES:(tile + 1) * LANES], tile)
+        tables(start[LANES:], 1)
+
+        @pl.when(me == 3)
+        def _():
+            tables(start[:LANES], 0)
 
         q_copy.wait()
 
@@ -649,24 +653,38 @@
 
     @pl.when(me == 2)
     def _():
-        for which, part in quarters:
-            near_out(which, part).wait_recv()
-            near_on(which, part).start()
-
-        @pl.loop(0, HK)
-        def _(head):
-            turn_key(head, 3)
-            for tile, (top, both) in enumerate(fresh(head, 3)):
-                keep(head, tile, top, both)
-
-        @pl.loop(0, HK)
-        def _(head):
-            mix_out(head).wait_recv()
-            mix_on(head).start()
-            turn(head, 2, mixed[head, 0], mixed[head, 1])
-            found = [scores_of(head, tile, 2, 3) for tile in range(2)]
-            for tile in range(2):
-                keep(head, tile, *more(head, tile, found[tile], 2, 3))
+        @pl.loop(0, HK // 2)
+        def _(part):
+            for which in range(2):
+                near_out(which, part).wait_recv()
+                near_on(which, part).start()
+
+            @pl.when(part == 1)
+            def _():
+                mix_out(0).wait_recv()
+                mix_on(0).start()
+
+            heads_now = [2 * part, 2 * part + 1]
+            for head in heads_now:
+                turn_key(head, 3)
+            results = fresh(heads_now, 3)
+            for at, (top, both) in enumerate(results):
+                keep(heads_now[at // 2], at % 2, top, both)
+
+        @pl.loop(0, HK // 2)
+        def _(part):
+            heads_now = [2 * part, 2 * part + 1]
+            for head in heads_now:
+                @pl.when(head > 0)
+                def _():
+                    mix_out(head).wait_recv()
+                    mix_on(head).start()
+
+            for head in heads_now:
+                turn(head, 2, mixed[head, 0], mixed[head, 1])
+            found = [scores_of(head, tile, 2, 3) for head in heads_now for tile in range(2)]
+            for at, scores in enumerate(found):
+                keep(heads_now[at // 2], at % 2, *more(heads_now[at // 2], at % 2, scores, 2, 3))
 
         @pl.loop(0, HK)
         def _(head):

time: 15.5 us -> 14.4 us (0.929)
  Pallas kernels: 14.4 us -> 13.2 us
    pallas_call x1, Pallas kernels: 14.4 us -> 13.2 us  [relay(): pl.pallas_call(relay_kernel, out_shape=pltpu.VMEM(queries.shape, BF16), i...]
where the time goes in v3:
time: 14.4 us; the launch traced here: 14.2 us
  Pallas kernels  13.2 us (92%)
  local copies, waits for them, and re-layouts  0.97 us (7%)
    pallas_call x1, Pallas kernels, relay(): pl.pallas_call(relay_kernel, out_shape=pltpu.VMEM(queries.shape, BF16), i...  13.2 us
    unnamed x1, local copies, waits for them, and re-layouts  0.97 us

profile of v3, /device:TPU:28, one launch (start us, length us, event | category | flops | bytes accessed | tf_op | source)
XLA Modules:
  0.0 14.2 jit_solution(14506249235829829283)
XLA Ops:
  0.0 13.2 %attend.1 = bf16[1,256,2048]{2,1,0:T(8,128)(2,1)S(1)} custom-call(bf16[1,256,2048]{2,1,0:T(8,128)(2,1)} %q_ref.1, bf16[1,256,512]{2,1,0:T(8,128)(2,1)} %k_ref.1, bf16[1,256,512]{2,1,0:T(8,128)(2,1)} %v_ref.1, s32[1,256]{1,0:T(1,128)} %seg_ref.1), custom_call_target="tpu_custom_call" | custom-call | tf_op jit(solution)/shard_map/attend/pallas_call | solution.py:770
  13.2 1.0 %copy.6 = bf16[1,256,2048]{2,1,0:T(8,128)(2,1)} copy(bf16[1,256,2048]{2,1,0:T(8,128)(2,1)S(1)} %attend.1) | data formatting | bytes 2097152

commit v4 on v3

--- a/solution.py
+++ b/solution.py
@@ -300,7 +300,7 @@
     sources = (k_ref, v_ref)
     own, before, after = blocks(4, 6), blocks(2, 4), blocks(6, 8)
     own_copies = [
-        pltpu.make_async_copy(sources[which].at[0], win.at[which, own], own_sem.at[which]) for which in range(2)
+        pltpu.make_async_copy(sources[which].at[0], win.at[which, own], own_sem) for which in range(2)
     ]
     seg_copy = pltpu.make_async_copy(seg_ref, segwin.at[2], seg_sem)
     q_copy = pltpu.make_async_copy(q_ref.at[0], q_own, q_sem)
@@ -336,10 +336,10 @@
         return remote(segwin.at[2], segwin.at[1], seg_send.at[2], seg_recv.at[2], me - 1)
 
     def own_out(which):
-        return remote(sources[which].at[0], win.at[which, before], own_send, own_recv.at[which], me + 1)
+        return remote(sources[which].at[0], win.at[which, before], own_send, own_recv, me + 1)
 
     def own_back(which):
-        return remote(sources[which].at[0], win.at[which, after], back_send, back_recv.at[which], me - 1)
+        return remote(sources[which].at[0], win.at[which, after], back_send, back_recv, me - 1)
 
     helped = pl.ds(0, (HK - 1) * group * HD)
 
@@ -349,20 +349,20 @@
     def give_out(head):
         width = group * HD
         at = pl.ds(head * width if isinstance(head, int) else pl.multiple_of(head * width, width), width)
-        return remote(next_out.at[:, at], out_ref.at[0, :, at], give_send, give_recv.at[head], me + 1)
+        return remote(next_out.at[:, at], out_ref.at[0, :, at], give_send, give_recv, me + 1)
 
     quarters = [(which, part) for part in range(2) for which in range(2)]
 
     def near_out(which, part):
         return remote(
             sources[which].at[0, blocks(1, 2), duo(part)], win.at[which, blocks(3, 4), duo(part)],
-            near_send, near_recv.at[which, part], me + 1,
+            near_send, near_recv.at[part], me + 1,
         )
 
     def near_on(which, part):
         return remote(
             win.at[which, blocks(3, 4), duo(part)], win.at[which, blocks(1, 2), duo(part)],
-            near_send, near_recv.at[which, part], me + 1,
+            near_send, near_recv.at[part], me + 1,
         )
 
     def mix_out(pair):
@@ -381,6 +381,9 @@
 
     def all_sent(ref, sent, received):
         remote(ref, ref, sent, received, me + 1).wait_send()
+
+    def all_here(ref, sent, received):
+        remote(ref, ref, sent, received, me + 1).wait_recv()
 
     freq = frequencies()
     lane = lax.broadcasted_iota(jnp.int32, (LANES, LANES), 1)
@@ -415,6 +418,11 @@
         at = blocks(block, block + 1)
         krot[head, at] = turned(keys, cosines[at], sines[at])
         vturn[head, 0:HD, at] = values.T
+
+    def place_piece(head, block, piece):
+        at = blocks(block, block + 1)
+        krot[head, at] = mixed[piece, 0]
+        vturn[head, 0:HD, at] = mixed[piece, 1]
 
     def turn_key(head, block):
         at = blocks(block, block + 1)
@@ -477,6 +485,11 @@
         weight = jnp.exp2((scores - top) * scale)
         return top, totals[head, tile] * ratio + summed(head, weight, blocks(first, last))
 
+    @pl.when(me == 2)
+    def _():
+        for pair in range(heads // 2):
+            q_back(pair).start()
+
     seg_copy.wait()
     for distance in (1, 2):
         @pl.when(me + distance < count)
@@ -486,11 +499,6 @@
     @pl.when(me == 1)
     def _():
         seg_back().start()
-
-    @pl.when(me == 2)
-    def _():
-        for pair in range(heads // 2):
-            q_back(pair).start()
 
     @pl.when(me == 1)
     def _():
@@ -529,8 +537,7 @@
         def _():
             seg_out(distance).wait_recv()
 
-    for which in range(2):
-        own_copies[which].wait()
+    pltpu.make_async_copy(win.at[:, own], win.at[:, own], own_sem).wait()
 
     pieces = []
     for index in range(3):
@@ -557,13 +564,14 @@
         seen = blocks(2, 5)
         for head in range(HK):
             turn_key(head, 4)
-        for which in range(2):
-            own_out(which).wait_recv()
+        all_here(win.at[:, before], own_send, own_recv)
+
+        for head in range(HK):
+            turn_key(head, 2)
+            turn_key(head, 3)
 
         @pl.loop(0, HK)
         def _(head):
-            turn_key(head, 2)
-            turn_key(head, 3)
             for part in range(group // 2):
                 pair = 2 * head + part
                 q_back(pair).wait_recv()
@@ -580,17 +588,18 @@
                 under = both[HD:HD + 1]
                 total = both[:HD] * (1.0 / under)
                 place = blocks(4 - pair // HK, None)
+                held = (krot[pair % HK, place], vturn[pair % HK, 0:HD, place])
                 for member in range(2):
                     mix[pair, member] = jnp.where(
-                        given, total[:, member * LANES:(member + 1) * LANES],
-                        win[member, place, columns(pair % HK)].astype(F32),
+                        given, total[:, member * LANES:(member + 1) * LANES], held[member].astype(F32)
                     ).astype(BF16)
                 lse = top + jnp.log(under) * F32(math.sqrt(HD))
                 for member in range(2):
                     at = 2 * part + member
                     lse_out[head, at:at + 1] = lse[:, member * LANES:(member + 1) * LANES]
+                if part == group // 2 - 1:
+                    lse_copy(head).start()
                 mix_out(pair).start()
-            lse_copy(head).start()
 
     tables(begin[LANES:], 5)
     mark[...] = begin[:LANES].T[:8]
@@ -621,8 +630,7 @@
             for tile, (top, both) in enumerate(fresh(head, 4)):
                 put(head, tile, both[:HD], both[HD:HD + 1])
 
-        for which in range(2):
-            own_back(which).wait_recv()
+        all_here(win.at[:, after], back_send, back_recv)
         help_out().wait_recv()
 
         @pl.loop(0, HK - 1)
@@ -636,12 +644,9 @@
 
     @pl.when(me >= 2)
     def _():
-        start = start_of(0, pieces)
-        tables(start[LANES:], 1)
-
         @pl.when(me == 3)
         def _():
-            tables(start[:LANES], 0)
+            tables(start_of(0, pieces)[LANES:], 1)
 
         q_copy.wait()
 
@@ -655,8 +660,8 @@
     def _():
         @pl.loop(0, HK // 2)
         def _(part):
+            all_here(win.at[:, blocks(3, 4), duo(part)], near_send, near_recv.at[part])
             for which in range(2):
-                near_out(which, part).wait_recv()
                 near_on(which, part).start()
 
             @pl.when(part == 1)
@@ -681,7 +686,7 @@
                     mix_on(head).start()
 
             for head in heads_now:
-                turn(head, 2, mixed[head, 0], mixed[head, 1])
+                place_piece(head, 2, head)
             found = [scores_of(head, tile, 2, 3) for head in heads_now for tile in range(2)]
             for at, scores in enumerate(found):
                 keep(heads_now[at // 2], at % 2, *more(heads_now[at // 2], at % 2, scores, 2, 3))
@@ -690,7 +695,7 @@
         def _(head):
             mix_out(HK + head).wait_recv()
             lse_copy(head).wait_recv()
-            turn(head, 1, mixed[HK + head, 0], mixed[HK + head, 1])
+            place_piece(head, 1, HK + head)
             found = [scores_of(head, tile, 1, 2) for tile in range(2)]
             crossing = spread(mark[0:1] < F32(LANES))
             lse = jnp.concatenate([lse_in[head, member:member + 1] for member in range(group)], axis=1)
@@ -706,8 +711,7 @@
 
     @pl.when(me == 3)
     def _():
-        for which in range(2):
-            own_out(which).wait_recv()
+        all_here(win.at[:, before], own_send, own_recv)
 
         @pl.loop(0, HK)
         def _(head):
@@ -716,13 +720,13 @@
             for tile, (top, both) in enumerate(fresh(head, 2)):
                 keep(head, tile, top, both)
 
-        for which, part in quarters:
-            near_on(which, part).wait_recv()
+        for part in range(2):
+            all_here(win.at[:, blocks(1, 2), duo(part)], near_send, near_recv.at[part])
 
         @pl.loop(0, HK)
         def _(head):
             mix_on(head).wait_recv()
-            turn(head, 0, mixed[head, 0], mixed[head, 1])
+            place_piece(head, 0, head)
             turn_key(head, 1)
             found = [scores_of(head, tile, tile, 2) for tile in range(2)]
             for tile in range(2):
@@ -736,26 +740,25 @@
 
     @pl.when(me % 2 == 0)
     def _():
-        all_sent(win.at[:, own], own_send, own_recv.at[0])
+        all_sent(win.at[:, own], own_send, own_recv)
 
     @pl.when(me == 0)
     def _():
-        all_sent(next_out.at[:, helped], give_send, give_recv.at[0])
+        all_sent(next_out.at[:, helped], give_send, give_recv)
 
     @pl.when(me == 1)
     def _():
         seg_back().wait_send()
-        all_sent(win.at[:, blocks(3, 4)], near_send, near_recv.at[0, 0])
-        all_sent(win.at[:, own], back_send, back_recv.at[0])
+        all_sent(win.at[:, blocks(3, 4)], near_send, near_recv.at[0])
+        all_sent(win.at[:, own], back_send, back_recv)
         help_out().wait_send()
         all_sent(mix, mix_send, mix_recv.at[0])
         all_sent(lse_out.at[:, few], lse_send, lse_recv.at[0])
-        for head in range(HK - 1):
-            give_out(head).wait_recv()
+        all_here(out_ref.at[0, :, helped], give_send, give_recv)
 
     @pl.when(me == 2)
     def _():
-        all_sent(win.at[:, blocks(3, 4)], near_send, near_recv.at[0, 0])
+        all_sent(win.at[:, blocks(3, 4)], near_send, near_recv.at[0])
         all_sent(mixed.at[pl.ds(0, HK)], mix_send, mix_recv.at[0])
         all_sent(q_own.at[blocks(0, 1)], q_send, q_recv.at[0])
 
@@ -797,9 +800,9 @@
             pltpu.VMEM((HK, 2, stack, HD), BF16),
             pltpu.VMEM((2, width + rows, LANES), F32),
             pltpu.VMEM((rows, heads * HD), BF16),
-            dma, dma, dma((2,)), dma((3,)), dma((3,)), dma, dma((2,)), dma, dma((2,)),
-            dma, dma((2, 2)), dma, dma((heads // 2,)), dma, dma((HK,)), dma, dma((heads // 2,)),
-            dma, dma, dma, dma((HK - 1,)),
+            dma, dma, dma, dma((3,)), dma((3,)), dma, dma, dma, dma,
+            dma, dma((2,)), dma, dma((heads // 2,)), dma, dma((HK,)), dma, dma((heads // 2,)),
+            dma, dma, dma, dma,
         ],
         compiler_params=pltpu.CompilerParams(
             collective_id=0, has_side_effects=True, vmem_limit_bytes=60 * 1024 * 1024

time: 14.4 us -> 14.1 us (0.979)
  Pallas kernels: 13.2 us -> 13 us
    pallas_call x1, Pallas kernels: 13.2 us -> 13 us  [relay(): pl.pallas_call(relay_kernel, out_shape=pltpu.VMEM(queries.shape, BF16), i...]
where the time goes in v4:
time: 14.1 us; the launch traced here: 14 us
  Pallas kernels  13 us (92%)
  local copies, waits for them, and re-layouts  0.97 us (7%)
    pallas_call x1, Pallas kernels, relay(): pl.pallas_call(relay_kernel, out_shape=pltpu.VMEM(queries.shape, BF16), i...  13 us
    unnamed x1, local copies, waits for them, and re-layouts  0.97 us

profile of v4, /device:TPU:28, one launch (start us, length us, event | category | flops | bytes accessed | tf_op | source)
XLA Modules:
  0.0 14.0 jit_solution(18310753635042306908)
XLA Ops:
  0.0 13.0 %attend.1 = bf16[1,256,2048]{2,1,0:T(8,128)(2,1)S(1)} custom-call(bf16[1,256,2048]{2,1,0:T(8,128)(2,1)} %q_ref.1, bf16[1,256,512]{2,1,0:T(8,128)(2,1)} %k_ref.1, bf16[1,256,512]{2,1,0:T(8,128)(2,1)} %v_ref.1, s32[1,256]{1,0:T(1,128)} %seg_ref.1), custom_call_target="tpu_custom_call" | custom-call | tf_op jit(solution)/shard_map/attend/pallas_call | solution.py:773
  13.0 1.0 %copy.6 = bf16[1,256,2048]{2,1,0:T(8,128)(2,1)} copy(bf16[1,256,2048]{2,1,0:T(8,128)(2,1)S(1)} %attend.1) | data formatting | bytes 2097152

commit v5 on v4

--- a/solution.py
+++ b/solution.py
@@ -379,6 +379,17 @@
     def q_back(pair):
         return remote(q_ref.at[0, blocks(0, 1), duo(pair)], q_in.at[pair], q_send, q_recv.at[pair], me - 1)
 
+    final = heads // 2 - 1
+
+    def q_half(member):
+        return remote(
+            q_ref.at[0, blocks(0, 1), columns(2 * final + member)], q_in.at[final, :, columns(member)],
+            q_send, q_recv.at[final + member], me - 1,
+        )
+
+    def mix_half(member):
+        return remote(mix.at[final, member], mixed.at[final, member], mix_send, mix_recv.at[final], me + 1)
+
     def all_sent(ref, sent, received):
         remote(ref, ref, sent, received, me + 1).wait_send()
 
@@ -487,8 +498,10 @@
 
     @pl.when(me == 2)
     def _():
-        for pair in range(heads // 2):
+        for pair in range(heads // 2 - 1):
             q_back(pair).start()
+        for member in range(2):
+            q_half(member).start()
 
     seg_copy.wait()
     for distance in (1, 2):
@@ -570,36 +583,44 @@
             turn_key(head, 2)
             turn_key(head, 3)
 
-        @pl.loop(0, HK)
+        def serve(head, part, members):
+            pair = 2 * head + part
+            turns = [
+                turned(q_in[pair, :, member * HD:(member + 1) * HD], q_cosine[...], q_sine[...]) for member in members
+            ]
+            scores = raw_scores(krot[head, seen], jnp.concatenate(turns, axis=0))
+            scores = scores + jnp.concatenate([q_bias[...]] * len(members), axis=1)
+            top = jnp.max(scores, axis=0, keepdims=True)
+            both = summed(head, jnp.exp2((scores - top) * scale), seen)
+            under = both[HD:HD + 1]
+            total = both[:HD] * (1.0 / under)
+            place = blocks(4 - pair // HK, None) if not isinstance(pair, int) else blocks(4 - pair // HK, 5 - pair // HK)
+            held = (krot[pair % HK, place], vturn[pair % HK, 0:HD, place])
+            lse = top + jnp.log(under) * F32(math.sqrt(HD))
+            for index, member in enumerate(members):
+                mine = slice(index * LANES, (index + 1) * LANES)
+                mix[pair, member] = jnp.where(given, total[:, mine], held[member].astype(F32)).astype(BF16)
+                at = 2 * part + member
+                lse_out[head, at:at + 1] = lse[:, mine]
+
+        @pl.loop(0, HK - 1)
         def _(head):
             for part in range(group // 2):
-                pair = 2 * head + part
-                q_back(pair).wait_recv()
-                one = jnp.concatenate(
-                    [
-                        turned(q_in[pair, :, member * HD:(member + 1) * HD], q_cosine[...], q_sine[...])
-                        for member in range(2)
-                    ],
-                    axis=0,
-                )
-                scores = raw_scores(krot[head, seen], one) + jnp.concatenate([q_bias[...]] * 2, axis=1)
-                top = jnp.max(scores, axis=0, keepdims=True)
-                both = summed(head, jnp.exp2((scores - top) * scale), seen)
-                under = both[HD:HD + 1]
-                total = both[:HD] * (1.0 / under)
-                place = blocks(4 - pair // HK, None)
-                held = (krot[pair % HK, place], vturn[pair % HK, 0:HD, place])
-                for member in range(2):
-                    mix[pair, member] = jnp.where(
-                        given, total[:, member * LANES:(member + 1) * LANES], held[member].astype(F32)
-                    ).astype(BF16)
-                lse = top + jnp.log(under) * F32(math.sqrt(HD))
-                for member in range(2):
-                    at = 2 * part + member
-                    lse_out[head, at:at + 1] = lse[:, member * LANES:(member + 1) * LANES]
+                q_back(2 * head + part).wait_recv()
+                serve(head, part, [0, 1])
                 if part == group // 2 - 1:
                     lse_copy(head).start()
-                mix_out(pair).start()
+                mix_out(2 * head + part).start()
+
+        q_back(heads // 2 - 2).wait_recv()
+        serve(HK - 1, 0, [0, 1])
+        mix_out(heads // 2 - 2).start()
+        for member in range(2):
+            q_half(member).wait_recv()
+            serve(HK - 1, 1, [member])
+            if member == 1:
+                lse_copy(HK - 1).start()
+            mix_half(member).start()
 
     tables(begin[LANES:], 5)
     mark[...] = begin[:LANES].T[:8]
@@ -801,7 +822,7 @@
             pltpu.VMEM((2, width + rows, LANES), F32),
             pltpu.VMEM((rows, heads * HD), BF16),
             dma, dma, dma, dma((3,)), dma((3,)), dma, dma, dma, dma,
-            dma, dma((2,)), dma, dma((heads // 2,)), dma, dma((HK,)), dma, dma((heads // 2,)),
+            dma, dma((2,)), dma, dma((heads // 2,)), dma, dma((HK,)), dma, dma((heads // 2 + 1,)),
             dma, dma, dma, dma,
         ],
         compiler_params=pltpu.CompilerParams(

time: 14.1 us -> 14.1 us (level)
  no operation moved by 1% of the time
where the time goes in v5:
time: 14.1 us; the launch traced here: 14 us
  Pallas kernels  13 us (92%)
  local copies, waits for them, and re-layouts  0.97 us (7%)
    pallas_call x1, Pallas kernels, relay(): pl.pallas_call(relay_kernel, out_shape=pltpu.VMEM(queries.shape, BF16), i...  13 us
    unnamed x1, local copies, waits for them, and re-layouts  0.97 us

profile of v5, /device:TPU:28, one launch (start us, length us, event | category | flops | bytes accessed | tf_op | source)
XLA Modules:
  0.0 14.0 jit_solution(11725871192965991280)
XLA Ops:
  0.0 13.0 %attend.1 = bf16[1,256,2048]{2,1,0:T(8,128)(2,1)S(1)} custom-call(bf16[1,256,2048]{2,1,0:T(8,128)(2,1)} %q_ref.1, bf16[1,256,512]{2,1,0:T(8,128)(2,1)} %k_ref.1, bf16[1,256,512]{2,1,0:T(8,128)(2,1)} %v_ref.1, s32[1,256]{1,0:T(1,128)} %seg_ref.1), custom_call_target="tpu_custom_call" | custom-call | tf_op jit(solution)/shard_map/attend/pallas_call | solution.py:794
  13.0 1.0 %copy.6 = bf16[1,256,2048]{2,1,0:T(8,128)(2,1)} copy(bf16[1,256,2048]{2,1,0:T(8,128)(2,1)S(1)} %attend.1) | data formatting | bytes 2097152
